TPU v7x, 32 devices: a whole 2x2x4 slice. The times are simulated.
32 devices in a mesh: grp: 1, dev: 32 (over z, y, x, core).
Axes of the slice: x: 2, y: 2, z: 4, core: 2. Of those that a mesh axis runs over, the one named last changes fastest.
Arguments:
- points: float32 [32768, 768], P(('grp', 'dev')), may hold values from -12 to 12
- assignment: int32 [32768], P(('grp', 'dev')), may hold values from 0 to 8191, as said below
Outputs:
- centroids: float32 [8192, 768], P('dev')
- spread: float32 [8192], P('dev')
Inputs may be any that keep to these rules, and one draw needn't show every extreme that they name: `assignment`: the owner of cluster c is c // 256. Among the 1024 points of one device (aligned blocks of 1024), at most 64 belong to clusters of one owner; some owner receives exactly 64 from every device's block.
All inputs are finite; a program needn't handle non-finite values.
Results may differ from a plain program's by a relative error of at most 0.000071.
Values sent between devices are 32-bit elements; how exact they have to be, the bound alone decides.
A program may use at most 64 MiB of HBM per device.

v0:
```python
import jax
import jax.numpy as jnp
from jax import lax
from jax.sharding import PartitionSpec as P

CL_OWN = 256


def finish(sums, counts, squares):
    denom = jnp.maximum(counts, 1.0)
    centre = sums / denom[:, None]
    spread = (squares - jnp.sum(sums * sums, axis=1) / denom) / (denom * sums.shape[1])
    return (centre, spread)


def body(points, assignment):
    owners = lax.axis_size("dev")
    rows, width = points.shape
    capacity = 2 * rows // owners
    owner = assignment // CL_OWN
    local_label = assignment % CL_OWN
    matches = (owner[:, None] == jnp.arange(owners, dtype=jnp.int32)[None, :]).astype(jnp.float32)
    earlier = (jnp.arange(rows)[:, None] > jnp.arange(rows)[None, :]).astype(jnp.float32)
    before = jnp.dot(earlier, matches, preferred_element_type=jnp.float32)
    position = jnp.sum(before * matches, axis=1).astype(jnp.int32)
    target = owner * capacity + position
    outgoing = jnp.zeros((owners * capacity, width), jnp.float32).at[target].set(points)
    labels = jnp.full((owners * capacity,), -1, jnp.int32).at[target].set(local_label)
    arrived, tags = (
        lax.all_to_all(
            outgoing.reshape(owners, capacity, width),
            "dev",
            split_axis=0,
            concat_axis=0,
            tiled=True,
        ),
        lax.all_to_all(
            labels.reshape(owners, capacity), "dev", split_axis=0, concat_axis=0, tiled=True
        ),
    )
    arrived = arrived.reshape(owners * capacity, width)
    tags = tags.reshape(owners * capacity)
    onehot = (jnp.arange(CL_OWN, dtype=jnp.int32)[:, None] == tags[None, :]).astype(jnp.float32)
    sums = jnp.dot(
        onehot, arrived, precision=lax.Precision.HIGHEST, preferred_element_type=jnp.float32
    )
    counts = jnp.sum(onehot, axis=1)
    squares = jnp.dot(
        onehot,
        jnp.sum(arrived * arrived, axis=1),
        precision=lax.Precision.HIGHEST,
        preferred_element_type=jnp.float32,
    )
    sums, counts, squares = lax.psum((sums, counts, squares), "grp")
    centre, spread = finish(sums, counts, squares)
    return (centre, spread)


def solution(mesh):
    return jax.shard_map(
        body,
        mesh=mesh,
        in_specs=(P(("grp", "dev"), None), P(("grp", "dev"))),
        out_specs=(P("dev", None), P("dev")),
        check_vma=False,
    )
```

profile of v0, /device:TPU:0, one launch (start us, length us, event | category | flops | bytes accessed | tf_op | source)
XLA Modules:
  0.0 181.4 jit_solution(455551329363810972)
XLA Ops:
  0.6 0.7 add_select_fusion.1
  1.3 0.5 fusion.6
  1.9 0.7 add_select_fusion
  2.6 4.3 %scatter_custom_fusion = s32[2048]{0:T(1024)S(1)} fusion(s32[1024]{0:T(1024)S(1)} %get-tuple-element.5, s32[1024]{0:T(1024)S(1)} %get-tuple-element.4, s32[]{:T(128)} %constant.31.clone.1), kind=kCustom, calls=%fused_computation.26 | custom fusion | bytes 8196 | tf_op jit(solution)/shard_map/scatter | solution.py:28
  6.9 0.7 all_to_all.9
  7.6 7.3 %all-to-all-start = ((s32[32,1,64]{2,1,0:T(1,128)}), s32[32,1,64]{2,1,0:T(1,128)S(1)}, u32[]{:S(2)}, u32[]{:S(2)}) async-start(s32[32,1,64]{2,1,0:T(1,128)} %all_to_all.9), calls=%async_computation | async-start | bytes 32768 | tf_op jit(solution)/shard_map/all_to_all | solution.py:37
  14.9 8.7 %scatter_custom_fusion.1 = f32[2048,768]{1,0:T(8,128)} fusion(s32[1024]{0:T(1024)S(1)} %get-tuple-element.5, f32[1024,768]{1,0:T(8,128)} %param.2, f32[]{:T(128)} %constant.37.clone.1), kind=kCustom, calls=%fused_computation.5 | custom fusion | bytes 6291968 | tf_op jit(solution)/shard_map/scatter | solution.py:27
  23.6 0.0 all-to-all-done
  23.6 5.9 %all-to-all-start.1 = ((f32[32,64,768]{2,1,0:T(8,128)}), f32[32,64,768]{2,1,0:T(8,128)}, u32[]{:S(2)}, u32[]{:S(2)}) async-start(f32[32,64,768]{2,1,0:T(8,128)} %bitcast.7), calls=%async_computation.1 | async-start | bytes 12582912 | tf_op jit(solution)/shard_map/all_to_all | solution.py:30
  29.5 0.5 broadcast.36
  30.0 0.7 reduce.4
  30.7 0.1 eq.34
  30.8 0.3 convert_reduce_fusion
  31.1 138.2 %all-to-all-done.1 = f32[32,64,768]{2,1,0:T(8,128)} async-done(((f32[32,64,768]{2,1,0:T(8,128)}), f32[32,64,768]{2,1,0:T(8,128)}, u32[]{:S(2)}, u32[]{:S(2)}) %all-to-all-start.1) | async-done | bytes 6291488 | tf_op jit(solution)/shard_map/all_to_all | solution.py:30
  169.3 3.3 %multiply_reduce_fusion = f32[32,64]{1,0:T(8,128)S(1)} fusion(f32[32,64,768]{2,1,0:T(8,128)} %all-to-all-done.1), kind=kLoop, calls=%fused_computation.2 | loop fusion | flops 3143680 | bytes 6299648 | tf_op jit(solution)/shard_map/reduce_sum | solution.py:50
  172.5 0.1 reshape.41
  172.6 1.0 fusion.3
  173.6 7.2 %multiply_reduce_fusion.1 = (f32[256]{0:T(256)S(1)}, f32[256,768]{1,0:T(8,128)}) fusion(f32[256]{0:T(256)S(1)} %broadcast_maximum_fusion, f32[2048,768]{1,0:T(8,128)} %bitcast.1, s32[2048]{0:T(1024)S(1)} %eq.34), kind=kOutput, calls=%fused_computation.15 | convolution fusion | flops 4832952320 | bytes 7088128 | tf_op jit(solution)/shard_map/dot_general | solution.py:44
  180.8 0.6 multiply_divide_fusion
  (1 shorter events, 0.0 us)
Async XLA Ops:
  7.6 16.0 %all-to-all-start = ((s32[32,1,64]{2,1,0:T(1,128)}), s32[32,1,64]{2,1,0:T(1,128)S(1)}, u32[]{:S(2)}, u32[]{:S(2)}) async-start(s32[32,1,64]{2,1,0:T(1,128)} %all_to_all.9), calls=%async_computation | async-start | bytes 32768 | tf_op jit(solution)/shard_map/all_to_all | solution.py:37
  23.6 145.7 %all-to-all-start.1 = ((f32[32,64,768]{2,1,0:T(8,128)}), f32[32,64,768]{2,1,0:T(8,128)}, u32[]{:S(2)}, u32[]{:S(2)}) async-start(f32[32,64,768]{2,1,0:T(8,128)} %bitcast.7), calls=%async_computation.1 | async-start | bytes 12582912 | tf_op jit(solution)/shard_map/all_to_all | solution.py:30
where the time goes:
time: 182 us; the launch traced here: 181 us
  waiting for transfers between devices  138 us (76%)
  local copies, waits for them, and re-layouts  14.3 us (8%)
  starting transfers between devices  13.3 us (7%)
  matrix products  8.72 us (5%)
  other arithmetic  6.22 us (3%)
    all_to_all x1, waiting for transfers between devices, body(): lax.all_to_all(outgoing.reshape(owners, capacity, width), 'dev', split_ax...  138 us
    scatter x1, local copies, waits for them, and re-layouts, body(): jnp.zeros((owners * capacity, width), jnp.float32).at[target].set(points)  8.66 us
    all_to_all x1, starting transfers between devices, body(): lax.all_to_all(labels.reshape(owners, capacity), 'dev', split_axis=0, con...  7.32 us
    dot_general x1, matrix products, body(): jnp.dot(onehot, arrived, precision=lax.Precision.HIGHEST, preferred_eleme...  7.18 us
    all_to_all x1, starting transfers between devices, body(): lax.all_to_all(outgoing.reshape(owners, capacity, width), 'dev', split_ax...  5.95 us
    scatter x1, local copies, waits for them, and re-layouts, body(): jnp.full((owners * capacity,), -1, jnp.int32).at[target].set(local_label)  4.32 us
  transfers between devices with their start and end apart: 2, of which 1 were waited for; matrix products, arithmetic and copies ran while one was open for 6% of the time, Pallas kernels for 0%

commit v1 on v0

v1 whole, which is shorter than its diff:
```python
import functools

import jax
import jax.numpy as jnp
from jax import lax
from jax.experimental import pallas as pl
from jax.experimental.pallas import tpu as pltpu
from jax.sharding import PartitionSpec as P

CL_OWN = 256
LANES = 128
MESH = pl.DeviceIdType.MESH


def finish(sums, counts, squares):
    denom = jnp.maximum(counts, 1.0)
    centre = sums / denom[:, None]
    spread = (squares - jnp.sum(sums * sums, axis=1) / denom) / (denom * sums.shape[1])
    return (centre, spread)


def pieces(value, count):
    out = []
    for _ in range(count):
        part = value.astype(jnp.bfloat16)
        out.append(part)
        value = value - part.astype(jnp.float32)
    return out


def kernel(
    inner, outer, cap, order,
    points_ref, target_ref, meta_ref, sums_ref, aux_ref,
    high, low, out, got, got_meta, zout, zgot, zaux, zgot_aux,
    meta_send, meta_recv, send, recv, zsend, zrecv, zaux_send, zaux_recv,
):
    me = lax.axis_index("dev")
    plane = me // inner
    seat = lax.rem(me, inner)
    rows = points_ref.shape[0]
    width = points_ref.shape[1]
    rep = LANES // cap

    barrier = pltpu.get_barrier_semaphore()
    for d in range(1, inner):
        peer = plane * inner + lax.rem(seat + d, inner)
        pl.semaphore_signal(barrier, inc=1, device_id={"dev": peer}, device_id_type=MESH)
    for d in range(1, outer):
        peer = lax.rem(plane + d, outer) * inner + seat
        pl.semaphore_signal(barrier, inc=1, device_id={"dev": peer}, device_id_type=MESH)
    pl.semaphore_wait(barrier, inner + outer - 2)

    def meta_copy(d, source):
        p = lax.rem(seat + d, inner)
        s = lax.rem(seat + inner - d, inner) if source else seat
        return pltpu.make_async_remote_copy(
            src_ref=meta_ref.at[p],
            dst_ref=got_meta.at[s],
            send_sem=meta_send.at[d],
            recv_sem=meta_recv.at[d],
            device_id={"dev": plane * inner + p},
            device_id_type=MESH,
        )

    def data_copy(j, d, source):
        p = lax.rem(seat + d, inner)
        s = lax.rem(seat + inner - d, inner) if source else seat
        return pltpu.make_async_remote_copy(
            src_ref=out.at[j, p],
            dst_ref=got.at[j, s],
            send_sem=send.at[j, d],
            recv_sem=recv.at[j, d],
            device_id={"dev": plane * inner + p},
            device_id_type=MESH,
        )

    def z_copies(j):
        device = {"dev": lax.rem(plane + order[j], outer) * inner + seat}
        return (
            pltpu.make_async_remote_copy(
                src_ref=zout.at[j], dst_ref=zgot.at[j], send_sem=zsend.at[j], recv_sem=zrecv.at[j],
                device_id=device, device_id_type=MESH,
            ),
            pltpu.make_async_remote_copy(
                src_ref=zaux.at[j], dst_ref=zgot_aux.at[j], send_sem=zaux_send.at[j],
                recv_sem=zaux_recv.at[j], device_id=device, device_id_type=MESH,
            ),
        )

    for d in range(1, inner):
        meta_copy(d, False).start()

    value = points_ref[...]
    top = value.astype(jnp.bfloat16)
    high[...] = top
    low[...] = (value - top.astype(jnp.float32)).astype(jnp.bfloat16)

    for j in range(outer):
        k = lax.rem(plane + order[j], outer)
        slot = k * (inner * cap) + lax.broadcasted_iota(jnp.int32, (inner * cap, rows), 0)
        pick = (slot == target_ref[...]).astype(jnp.bfloat16)
        block = jnp.dot(pick, high[...], preferred_element_type=jnp.float32)
        block = block + jnp.dot(pick, low[...], preferred_element_type=jnp.float32)
        out[j] = block.reshape(inner, cap, width)
        for d in range(1, inner):
            data_copy(j, d, False).start()

    for d in range(1, inner):
        meta_copy(d, True).wait_recv()
    got_meta[seat] = meta_ref[seat]

    cluster = lax.broadcasted_iota(jnp.int32, (CL_OWN, LANES), 0).astype(jnp.float32)
    lane = lax.broadcasted_iota(jnp.int32, (1, LANES), 1)
    first = (lane < cap).astype(jnp.float32)
    for j in range(outer):
        k = lax.rem(plane + order[j], outer)
        hits, weights = [], []
        for s in range(inner):
            tags = got_meta[s, k, 0:1, :]
            hits.append((cluster == tags).astype(jnp.bfloat16))
            norms = got_meta[s, k, 1:2, :]
            weights.append(
                jnp.concatenate(
                    [first.astype(jnp.bfloat16)] + pieces(norms, 3)
                    + [jnp.zeros((4, LANES), jnp.bfloat16)],
                    axis=0,
                )
            )
        hit = jnp.concatenate(hits, axis=1)
        weight = jnp.concatenate(weights, axis=1)
        aux = lax.dot_general(
            weight, hit, (((1,), (1,)), ((), ())), preferred_element_type=jnp.float32
        )
        for d in range(1, inner):
            data_copy(j, d, True).wait_recv()
        got[j, seat] = out[j, seat]
        stack = []
        for s in range(inner):
            stack.extend(pieces(got[j, s], rep))
        total = jnp.dot(hit, jnp.concatenate(stack, axis=0), preferred_element_type=jnp.float32)
        if j < outer - 1:
            zaux[j] = aux
            zout[j] = total
            for copy in z_copies(j):
                copy.start()
        else:
            sums_ref[...] = total
            aux_ref[...] = aux

    for j in range(outer - 1):
        for copy in z_copies(j):
            copy.wait_recv()
        sums_ref[...] += zgot[j]
        aux_ref[...] += zgot_aux[j]

    for d in range(1, inner):
        meta_copy(d, False).wait_send()
        for j in range(outer):
            data_copy(j, d, False).wait_send()
    for j in range(outer - 1):
        for copy in z_copies(j):
            copy.wait_send()


def body(points, assignment):
    owners = lax.axis_size("dev")
    rows, width = points.shape
    cap = 2 * rows // owners
    inner = 1
    while 4 * inner * inner <= 2 * owners:
        inner *= 2
    outer = owners // inner
    order = sorted(range(1, outer), key=lambda d: (-min(d, outer - d), d)) + [0]

    owner = assignment // CL_OWN
    local_label = assignment % CL_OWN
    matches = (owner[:, None] == jnp.arange(owners, dtype=jnp.int32)[None, :]).astype(jnp.float32)
    earlier = (jnp.arange(rows)[:, None] > jnp.arange(rows)[None, :]).astype(jnp.float32)
    before = jnp.dot(earlier, matches, preferred_element_type=jnp.float32)
    position = jnp.sum(before * matches, axis=1).astype(jnp.int32)
    target = owner * cap + position

    norms = jnp.sum(points * points, axis=1)
    held = target[None, :] == jnp.arange(owners * cap, dtype=jnp.int32)[:, None]
    tags = jnp.sum(jnp.where(held, local_label[None, :] + 1, 0), axis=1) - 1
    slot_norms = jnp.sum(jnp.where(held, norms[None, :], 0.0), axis=1)
    tags = tags.astype(jnp.float32).reshape(outer, inner, 1, cap)
    slot_norms = slot_norms.reshape(outer, inner, 1, cap)
    meta = jnp.concatenate(
        [
            jnp.tile(tags, (1, 1, 1, LANES // cap)),
            jnp.pad(slot_norms, ((0, 0), (0, 0), (0, 0), (0, LANES - cap))),
            jnp.zeros((outer, inner, 6, LANES), jnp.float32),
        ],
        axis=2,
    ).transpose(1, 0, 2, 3)

    f32, b16 = jnp.float32, jnp.bfloat16
    dma = pltpu.SemaphoreType.DMA
    hops = max(outer - 1, 1)
    sums, aux = pl.pallas_call(
        functools.partial(kernel, inner, outer, cap, order),
        out_shape=(
            jax.ShapeDtypeStruct((CL_OWN, width), f32),
            jax.ShapeDtypeStruct((8, CL_OWN), f32),
        ),
        in_specs=[pl.BlockSpec(memory_space=pltpu.VMEM)] * 3,
        out_specs=[pl.BlockSpec(memory_space=pltpu.VMEM)] * 2,
        scratch_shapes=[
            pltpu.VMEM((rows, width), b16),
            pltpu.VMEM((rows, width), b16),
            pltpu.VMEM((outer, inner, cap, width), f32),
            pltpu.VMEM((outer, inner, cap, width), f32),
            pltpu.VMEM((inner, outer, 8, LANES), f32),
            pltpu.VMEM((hops, CL_OWN, width), f32),
            pltpu.VMEM((hops, CL_OWN, width), f32),
            pltpu.VMEM((hops, 8, CL_OWN), f32),
            pltpu.VMEM((hops, 8, CL_OWN), f32),
            dma((inner,)), dma((inner,)),
            dma((outer, inner)), dma((outer, inner)),
            dma((hops,)), dma((hops,)), dma((hops,)), dma((hops,)),
        ],
        compiler_params=pltpu.CompilerParams(
            collective_id=0, has_side_effects=True, vmem_limit_bytes=60 * 1024 * 1024
        ),
    )(points, target[None, :], meta)
    counts = aux[0]
    squares = aux[1] + aux[2] + aux[3]
    sums, counts, squares = lax.psum((sums, counts, squares), "grp")
    return finish(sums, counts, squares)


def solution(mesh):
    return jax.shard_map(
        body,
        mesh=mesh,
        in_specs=(P(("grp", "dev"), None), P(("grp", "dev"))),
        out_specs=(P("dev", None), P("dev")),
        check_vma=False,
    )
```

time: 182 us -> 108 us (0.59)
  waiting for transfers between devices: 138 us -> 0 us
  Pallas kernels: 0 us -> 97.9 us
  local copies, waits for them, and re-layouts: 14.3 us -> 0.37 us
  starting transfers between devices: 13.3 us -> 0 us
  matrix products: 8.72 us -> 0.53 us
  other arithmetic: 6.22 us -> 8.34 us
    all_to_all x2 -> x0, waiting for transfers between devices: 138 us -> none  [the longest x1 138 us: body(): lax.all_to_all(outgoing.reshape(owners, capacity, width), 'dev', split_ax...]
    pallas_call x0 -> x1, Pallas kernels: none -> 97.9 us  [body(): pl.pallas_call(functools.partial(kernel, inner, outer, cap, order), out_s...]
    all_to_all x2 -> x0, starting transfers between devices: 13.3 us -> none  [the longest x1 7.32 us: body(): lax.all_to_all(labels.reshape(owners, capacity), 'dev', split_axis=0, con...]
    scatter x2 -> x0, local copies, waits for them, and re-layouts: 13 us -> none  [the longest x1 8.66 us: body(): jnp.zeros((owners * capacity, width), jnp.float32).at[target].set(points)]
    dot_general x2 -> x0, matrix products: 8.19 us -> none  [the longest x1 7.18 us: body(): jnp.dot(onehot, arrived, precision=lax.Precision.HIGHEST, preferred_eleme...]
    reduce_sum x2 -> x4, other arithmetic: 3.55 us -> 6.15 us  [the longest x1 2.16 us: body(): norms = jnp.sum(points * points, axis=1)]
  transfers between devices with their start and end apart: 2 -> 0, of which waited for: 1 -> 0; matrix products, arithmetic and copies ran while one was open for 6% -> 0% of each run, Pallas kernels for 0% -> 0%
where the time goes in v1:
time: 108 us
  Pallas kernels  97.9 us (91%)
  other arithmetic  8.34 us (8%)
    pallas_call x1, Pallas kernels, body(): pl.pallas_call(functools.partial(kernel, inner, outer, cap, order), out_s...  97.9 us
    reduce_sum x1, other arithmetic, body(): norms = jnp.sum(points * points, axis=1)  2.16 us

profile of v1, /device:TPU:0, one launch (start us, length us, event | category | flops | bytes accessed | tf_op | source)
XLA Modules:
  0.0 107.8 jit_solution(13603844724858362312)
XLA Ops:
  0.6 0.0 copy-start.1
  0.6 0.1 pad.7.clone
  0.7 2.2 %multiply_reduce_fusion = f32[1024]{0:T(1024)S(1)} fusion(f32[1024,768]{1,0:T(8,128)} %points_ref.1), kind=kLoop, calls=%fused_computation.5 | loop fusion | flops 1571840 | bytes 3149824 | tf_op jit(solution)/shard_map/reduce_sum | solution.py:183
  2.9 0.0 copy-done.1
  2.9 0.5 fusion.2
  3.5 0.0 copy-start
  3.5 0.9 select_reduce_fusion.1
  4.4 0.9 select_reduce_fusion
  5.4 0.1 reshape.35
  5.5 0.1 convert_element_type.19
  5.5 0.1 tile.9
  5.7 0.7 fusion.4.meta_ref
  6.4 0.0 copy-done
  6.4 97.9 %shard_map.41 = (f32[256,768]{1,0:T(8,128)}, f32[8,256]{1,0:T(8,128)}) custom-call(f32[1024,768]{1,0:T(8,128)} %points_ref.1, s32[1,1024]{1,0:T(1,128)} %bitcast.7, f32[8,4,8,128]{3,2,1,0:T(8,128)} %fusion.4.meta_ref), custom_call_target="tpu_custom_call" | custom-call | tf_op jit(solution)/shard_map/pallas_call | solution.py:201
  104.3 0.9 slice_add_fusion
  105.1 2.1 %multiply_reduce_fusion.1 = (f32[256]{0:T(256)S(1)}, f32[256,768]{1,0:T(8,128)}) fusion(f32[256,768]{1,0:T(8,128)} %get-tuple-element.4, f32[256]{0:T(256)S(1)} %bitcast.8), kind=kLoop, calls=%fused_computation.8 | loop fusion | flops 589568 | bytes 1574912 | tf_op jit(solution)/shard_map/reduce_sum | solution.py:18
  107.3 0.6 multiply_divide_fusion
  (7 shorter events, 0.1 us)
Async XLA Ops:
  0.6 2.3 %copy-start.1 = (s32[1024]{0:T(1024)S(1)}, s32[1024]{0:T(1024)}, u32[]{:S(2)}) copy-start(s32[1024]{0:T(1024)} %param.3) | copy-start | bytes 12292
  3.5 2.9 %copy-start = (s32[1024]{0:T(1024)}, s32[1024]{0:T(1024)S(1)}, u32[]{:S(2)}) copy-start(s32[1024]{0:T(1024)S(1)} %get-tuple-element.11) | copy-start | bytes 12292

commit v2 on v0

v2 whole, which is shorter than its diff:
```python
import functools

import jax
import jax.numpy as jnp
from jax import lax
from jax.experimental import pallas as pl
from jax.experimental.pallas import tpu as pltpu
from jax.sharding import PartitionSpec as P

CL_OWN = 256
LANES = 128
MESH = pl.DeviceIdType.MESH


def finish(sums, counts, squares):
    denom = jnp.maximum(counts, 1.0)
    centre = sums / denom[:, None]
    spread = (squares - jnp.sum(sums * sums, axis=1) / denom) / (denom * sums.shape[1])
    return (centre, spread)


def pieces(value, count):
    out = []
    for _ in range(count):
        part = value.astype(jnp.bfloat16)
        out.append(part)
        value = value - part.astype(jnp.float32)
    return out


def kernel(
    inner, outer, cap, chunk,
    points_ref, route_ref, sums_ref, aux_ref,
    high, low, facts, hit, out, got, mout, mgot, zout, zin, zaux, zin_aux,
    msend, mrecv, send, recv, zsend, zrecv, asend, arecv,
):
    me = lax.axis_index("dev")
    plane = me // inner
    seat = lax.rem(me, inner)
    rows, width = points_ref.shape
    chunks = width // chunk
    rep = LANES // cap
    last = outer - 1
    rights, lefts = last - plane, plane

    def target_plane(j):
        if j == last:
            return plane
        right_first = jnp.where(j < rights, last - j, j - rights)
        left_first = jnp.where(j < lefts, j, last - j + lefts)
        return jnp.where(rights > lefts, right_first, left_first)

    def fed(j):
        k = target_plane(j)
        return jnp.where(k > plane, plane > 0, plane < last)

    barrier = pltpu.get_barrier_semaphore()
    for d in range(1, inner):
        peer = plane * inner + lax.rem(seat + d, inner)
        pl.semaphore_signal(barrier, inc=1, device_id={"dev": peer}, device_id_type=MESH)
    for d in range(1, outer):
        peer = lax.rem(plane + d, outer) * inner + seat
        pl.semaphore_signal(barrier, inc=1, device_id={"dev": peer}, device_id_type=MESH)
    pl.semaphore_wait(barrier, inner + outer - 2)

    def plane_copy(src, dst, ssem, rsem, index, d, arriving):
        p = lax.rem(seat + d, inner)
        s = lax.rem(seat + inner - d, inner) if arriving else seat
        return pltpu.make_async_remote_copy(
            src_ref=src.at[(*index, p)],
            dst_ref=dst.at[(*index, s)],
            send_sem=ssem.at[(*index, d)],
            recv_sem=rsem.at[(*index, d)],
            device_id={"dev": plane * inner + p},
            device_id_type=MESH,
        )

    def data_copy(j, c, d, arriving):
        return plane_copy(out, got, send, recv, (j, c), d, arriving)

    def meta_copy(j, d, arriving):
        return plane_copy(mout, mgot, msend, mrecv, (j,), d, arriving)

    def line_copy(j, c):
        k = target_plane(j)
        step = jnp.where(k > plane, 1, -1)
        place = jnp.where(k == plane - 1, outer, k)
        return pltpu.make_async_remote_copy(
            src_ref=zout.at[j, c],
            dst_ref=zin.at[place, c],
            send_sem=zsend.at[j, c],
            recv_sem=zrecv.at[place, c],
            device_id={"dev": (plane + step) * inner + seat},
            device_id_type=MESH,
        )

    def line_arrival(place, c):
        side = jnp.where(plane > 0, -1, 1)
        return pltpu.make_async_remote_copy(
            src_ref=zout.at[0, c],
            dst_ref=zin.at[place, c],
            send_sem=zsend.at[0, c],
            recv_sem=zrecv.at[place, c],
            device_id={"dev": (plane + side) * inner + seat},
            device_id_type=MESH,
        )

    def aux_copy(j, arriving):
        k = target_plane(j)
        return pltpu.make_async_remote_copy(
            src_ref=zaux.at[j],
            dst_ref=zin_aux.at[k if arriving else plane],
            send_sem=asend.at[j],
            recv_sem=arecv.at[k if arriving else plane],
            device_id={"dev": k * inner + seat},
            device_id_type=MESH,
        )

    def gather(j):
        slot = target_plane(j) * (inner * cap) + lax.broadcasted_iota(
            jnp.int32, (inner * cap, rows), 0
        )
        pick = (slot == route_ref[0:1, :]).astype(jnp.bfloat16)
        for c in range(chunks):
            columns = slice(c * chunk, (c + 1) * chunk)
            block = jnp.dot(pick, high[:, columns], preferred_element_type=jnp.float32)
            block = block + jnp.dot(pick, low[:, columns], preferred_element_type=jnp.float32)
            out[j, c] = block.reshape(inner, cap, chunk)
            for d in range(1, inner):
                data_copy(j, c, d, False).start()
        if j == 0:
            value = points_ref[...]
            norms = jnp.sum(value * value, axis=1, keepdims=True)
            norms = jnp.broadcast_to(norms, (rows, LANES)).T[0:1, :]
            label = route_ref[1:2, :].astype(jnp.float32).astype(jnp.bfloat16)
            blank = jnp.zeros((4, rows), jnp.bfloat16)
            facts[...] = jnp.concatenate([label] + pieces(norms, 3) + [blank], axis=0)
        told = lax.dot_general(
            facts[...], pick, (((1,), (1,)), ((), ())), preferred_element_type=jnp.float32
        )
        for p in range(inner):
            mine = told[:, p * cap : (p + 1) * cap]
            mout[j, p] = jnp.concatenate([mine] * rep, axis=1)
        for d in range(1, inner):
            meta_copy(j, d, False).start()

    lane = lax.broadcasted_iota(jnp.int32, (8, LANES), 1)
    line = lax.broadcasted_iota(jnp.int32, (8, LANES), 0)
    cluster = lax.broadcasted_iota(jnp.int32, (CL_OWN, LANES), 0).astype(jnp.float32) + 1.0

    def matches(j):
        for d in range(1, inner):
            meta_copy(j, d, True).wait_recv()
        mgot[j, seat] = mout[j, seat]
        weights = []
        for s in range(inner):
            block = mgot[j, s]
            hit[:, s * LANES : (s + 1) * LANES] = (cluster == block[0:1, :]).astype(jnp.bfloat16)
            block = jnp.where(line == 0, 1.0, block)
            weights.append(jnp.where(lane < cap, block, 0.0).astype(jnp.bfloat16))
        aux = lax.dot_general(
            jnp.concatenate(weights, axis=1), hit[...], (((1,), (1,)), ((), ())),
            preferred_element_type=jnp.float32,
        )
        if j < last:
            zaux[j] = aux
            aux_copy(j, False).start()
        else:
            aux_ref[...] = aux

    def reduce(j, c):
        for d in range(1, inner):
            data_copy(j, c, d, True).wait_recv()
        got[j, c, seat] = out[j, c, seat]
        stack = []
        for s in range(inner):
            stack.extend(pieces(got[j, c, s], rep))
        total = jnp.dot(hit[...], jnp.concatenate(stack, axis=0), preferred_element_type=jnp.float32)
        if j == last:
            sums_ref[:, c * chunk : (c + 1) * chunk] = total
        else:
            zout[j, c] = total

    def forward(j, c):
        @pl.when(fed(j))
        def _():
            k = target_plane(j)
            line_arrival(k, c).wait_recv()
            zout[j, c] += zin[k, c]
            line_copy(j, c).start()

    value = points_ref[...]
    top = value.astype(jnp.bfloat16)
    high[...] = top
    low[...] = (value - top.astype(jnp.float32)).astype(jnp.bfloat16)

    gather(0)
    behind = None
    for j in range(outer):
        if j == 0:
            for later in range(1, outer):
                gather(later)
        matches(j)
        for c in range(chunks):
            reduce(j, c)
            if j < last:
                @pl.when(jnp.logical_not(fed(j)))
                def _():
                    line_copy(j, c).start()
            if behind is not None:
                forward(*behind)
            behind = (j, c) if j < last else None

    for j in range(last):
        aux_copy(j, True).wait_recv()
        aux_ref[...] += zin_aux[target_plane(j)]
    for c in range(chunks):
        columns = slice(c * chunk, (c + 1) * chunk)

        @pl.when(plane > 0)
        def _():
            line_arrival(plane, c).wait_recv()
            sums_ref[:, columns] += zin[plane, c]

        @pl.when(plane < last)
        def _():
            line_arrival(outer, c).wait_recv()
            sums_ref[:, columns] += zin[outer, c]

    for j in range(outer):
        for d in range(1, inner):
            meta_copy(j, d, False).wait_send()
            for c in range(chunks):
                data_copy(j, c, d, False).wait_send()
    for j in range(last):
        aux_copy(j, False).wait_send()
        for c in range(chunks):
            line_copy(j, c).wait_send()


def body(points, assignment):
    owners = lax.axis_size("dev")
    rows, width = points.shape
    cap = 2 * rows // owners
    inner = 1
    while 4 * inner * inner <= 2 * owners:
        inner *= 2
    outer = owners // inner
    chunk = width // 3 if width % (3 * LANES) == 0 else width
    chunks = width // chunk

    owner = assignment // CL_OWN
    local_label = assignment % CL_OWN
    matches = (owner[:, None] == jnp.arange(owners, dtype=jnp.int32)[None, :]).astype(jnp.float32)
    earlier = (jnp.arange(rows)[:, None] > jnp.arange(rows)[None, :]).astype(jnp.float32)
    before = jnp.dot(earlier, matches, preferred_element_type=jnp.float32)
    position = jnp.sum(before * matches, axis=1).astype(jnp.int32)
    target = owner * cap + position
    route = jnp.stack([target, local_label + 1])

    f32, b16 = jnp.float32, jnp.bfloat16
    dma = pltpu.SemaphoreType.DMA
    hops = max(outer - 1, 1)
    sums, aux = pl.pallas_call(
        functools.partial(kernel, inner, outer, cap, chunk),
        out_shape=(
            jax.ShapeDtypeStruct((CL_OWN, width), f32),
            jax.ShapeDtypeStruct((8, CL_OWN), f32),
        ),
        in_specs=[pl.BlockSpec(memory_space=pltpu.VMEM)] * 2,
        out_specs=[pl.BlockSpec(memory_space=pltpu.VMEM)] * 2,
        scratch_shapes=[
            pltpu.VMEM((rows, width), b16),
            pltpu.VMEM((rows, width), b16),
            pltpu.VMEM((8, rows), b16),
            pltpu.VMEM((CL_OWN, inner * LANES), b16),
            pltpu.VMEM((outer, chunks, inner, cap, chunk), f32),
            pltpu.VMEM((outer, chunks, inner, cap, chunk), f32),
            pltpu.VMEM((outer, inner, 8, LANES), f32),
            pltpu.VMEM((outer, inner, 8, LANES), f32),
            pltpu.VMEM((hops, chunks, CL_OWN, chunk), f32),
            pltpu.VMEM((outer + 1, chunks, CL_OWN, chunk), f32),
            pltpu.VMEM((hops, 8, CL_OWN), f32),
            pltpu.VMEM((outer, 8, CL_OWN), f32),
            dma((outer, inner)), dma((outer, inner)),
            dma((outer, chunks, inner)), dma((outer, chunks, inner)),
            dma((hops, chunks)), dma((outer + 1, chunks)),
            dma((hops,)), dma((outer,)),
        ],
        compiler_params=pltpu.CompilerParams(
            collective_id=0, has_side_effects=True, vmem_limit_bytes=60 * 1024 * 1024
        ),
    )(points, route)
    counts = aux[0]
    squares = aux[1] + aux[2] + aux[3]
    sums, counts, squares = lax.psum((sums, counts, squares), "grp")
    return finish(sums, counts, squares)


def solution(mesh):
    return jax.shard_map(
        body,
        mesh=mesh,
        in_specs=(P(("grp", "dev"), None), P(("grp", "dev"))),
        out_specs=(P("dev", None), P("dev")),
        check_vma=False,
    )
```

time: 182 us -> 98.5 us (0.54)
  waiting for transfers between devices: 138 us -> 0 us
  Pallas kernels: 0 us -> 91.5 us
  local copies, waits for them, and re-layouts: 14.3 us -> 0 us
  starting transfers between devices: 13.3 us -> 0 us
  matrix products: 8.72 us -> 0.53 us
    all_to_all x2 -> x0, waiting for transfers between devices: 138 us -> none  [the longest x1 138 us: body(): lax.all_to_all(outgoing.reshape(owners, capacity, width), 'dev', split_ax...]
    pallas_call x0 -> x1, Pallas kernels: none -> 91.5 us  [body(): pl.pallas_call(functools.partial(kernel, inner, outer, cap, chunk), out_s...]
    all_to_all x2 -> x0, starting transfers between devices: 13.3 us -> none  [the longest x1 7.32 us: body(): lax.all_to_all(labels.reshape(owners, capacity), 'dev', split_axis=0, con...]
    scatter x2 -> x0, local copies, waits for them, and re-layouts: 13 us -> none  [the longest x1 8.66 us: body(): jnp.zeros((owners * capacity, width), jnp.float32).at[target].set(points)]
    dot_general x2 -> x0, matrix products: 8.19 us -> none  [the longest x1 7.18 us: body(): jnp.dot(onehot, arrived, precision=lax.Precision.HIGHEST, preferred_eleme...]
  transfers between devices with their start and end apart: 2 -> 0, of which waited for: 1 -> 0; matrix products, arithmetic and copies ran while one was open for 6% -> 0% of each run, Pallas kernels for 0% -> 0%
where the time goes in v2:
time: 98.5 us; the launch traced here: 98.2 us
  Pallas kernels  91.5 us (93%)
  other arithmetic  5.57 us (6%)
    pallas_call x1, Pallas kernels, body(): pl.pallas_call(functools.partial(kernel, inner, outer, cap, chunk), out_s...  91.5 us
    reduce_sum x1, other arithmetic, finish(): jnp.sum(sums * sums, axis=1) / denom  2.14 us

profile of v2, /device:TPU:0, one launch (start us, length us, event | category | flops | bytes accessed | tf_op | source)
XLA Modules:
  0.0 98.2 jit_solution(13838256174620659542)
XLA Ops:
  0.6 0.7 add_select_fusion.1
  1.3 0.5 fusion.2
  1.9 0.7 convert_add_fusion
  2.6 0.6 pad_add_fusion.route_ref
  3.2 91.5 %shard_map.41 = (f32[256,768]{1,0:T(8,128)}, f32[8,256]{1,0:T(8,128)}) custom-call(f32[1024,768]{1,0:T(8,128)} %points_ref.1, s32[2,1024]{1,0:T(2,128)} %pad_add_fusion.route_ref), custom_call_target="tpu_custom_call" | custom-call | tf_op jit(solution)/shard_map/pallas_call | solution.py:264
  94.6 0.9 slice_add_fusion
  95.5 2.1 %multiply_reduce_fusion = (f32[256]{0:T(256)S(1)}, f32[256,768]{1,0:T(8,128)}) fusion(f32[256,768]{1,0:T(8,128)} %get-tuple-element.4, f32[256]{0:T(256)S(1)} %bitcast.6), kind=kLoop, calls=%fused_computation.4 | loop fusion | flops 589568 | bytes 1574912 | tf_op jit(solution)/shard_map/reduce_sum | solution.py:18
  97.6 0.6 multiply_divide_fusion

commit v3 on v2

--- a/solution.py
+++ b/solution.py
@@ -31,8 +31,8 @@
 def kernel(
     inner, outer, cap, chunk,
     points_ref, route_ref, sums_ref, aux_ref,
-    high, low, facts, hit, out, got, mout, mgot, zout, zin, zaux, zin_aux,
-    msend, mrecv, send, recv, zsend, zrecv, asend, arecv,
+    high, low, facts, hit, out, got, relay, mout, mgot, zout, zin, zaux, zin_aux,
+    msend, mrecv, send, recv, rsend, rrecv, zsend, zrecv, asend, arecv,
 ):
     me = lax.axis_index("dev")
     plane = me // inner
@@ -54,32 +54,57 @@
         k = target_plane(j)
         return jnp.where(k > plane, plane > 0, plane < last)
 
+    def across(d):
+        other = 0
+        for bit in range(3):
+            own = lax.rem(seat // 2**bit, 2)
+            other = other + (1 - own if d // 2**bit % 2 else own) * 2**bit
+        return other
+
     barrier = pltpu.get_barrier_semaphore()
     for d in range(1, inner):
-        peer = plane * inner + lax.rem(seat + d, inner)
+        peer = plane * inner + across(d)
         pl.semaphore_signal(barrier, inc=1, device_id={"dev": peer}, device_id_type=MESH)
     for d in range(1, outer):
         peer = lax.rem(plane + d, outer) * inner + seat
         pl.semaphore_signal(barrier, inc=1, device_id={"dev": peer}, device_id_type=MESH)
-    pl.semaphore_wait(barrier, inner + outer - 2)
-
-    def plane_copy(src, dst, ssem, rsem, index, d, arriving):
-        p = lax.rem(seat + d, inner)
-        s = lax.rem(seat + inner - d, inner) if arriving else seat
+    def plane_copy(src, dst, ssem, rsem, d):
         return pltpu.make_async_remote_copy(
-            src_ref=src.at[(*index, p)],
-            dst_ref=dst.at[(*index, s)],
-            send_sem=ssem.at[(*index, d)],
-            recv_sem=rsem.at[(*index, d)],
-            device_id={"dev": plane * inner + p},
+            src_ref=src,
+            dst_ref=dst,
+            send_sem=ssem,
+            recv_sem=rsem,
+            device_id={"dev": plane * inner + across(d)},
             device_id_type=MESH,
         )
 
-    def data_copy(j, c, d, arriving):
-        return plane_copy(out, got, send, recv, (j, c), d, arriving)
+    def data_copy(j, c, d):
+        return plane_copy(
+            out.at[j, c, across(d)], got.at[j, c, seat], send.at[j, c, d], recv.at[j, c, d], d
+        )
+
+    def relay_out(j, c, d):
+        return plane_copy(
+            out.at[j, c, across(d)], relay.at[j, c, d - 6], rsend.at[j, c, d - 6],
+            rrecv.at[j, c, d - 6], 2,
+        )
+
+    def relay_on(j, c, d):
+        return plane_copy(
+            relay.at[j, c, d - 6], got.at[j, c, across(2)], send.at[j, c, d], recv.at[j, c, d],
+            d - 2,
+        )
+
+    def data_arrival(j, c, d):
+        return plane_copy(
+            out.at[j, c, 0], got.at[j, c, across(d)], send.at[j, c, d], recv.at[j, c, d], d
+        )
 
     def meta_copy(j, d, arriving):
-        return plane_copy(mout, mgot, msend, mrecv, (j,), d, arriving)
+        return plane_copy(
+            mout.at[j, across(d)], mgot.at[j, across(d) if arriving else seat],
+            msend.at[j, d], mrecv.at[j, d], d,
+        )
 
     def line_copy(j, c):
         k = target_plane(j)
@@ -116,6 +141,20 @@
             device_id_type=MESH,
         )
 
+    steps = outer * chunks
+    ahead = min(2, steps)
+
+    def own_y(t):
+        for d in (4, 5):
+            data_copy(t // chunks, t % chunks, d).start()
+
+    def pass_on(t):
+        for d in (6, 7):
+            relay_out(t // chunks, t % chunks, d).wait_recv()
+            relay_on(t // chunks, t % chunks, d).start()
+        if t + ahead < steps:
+            own_y(t + ahead)
+
     def gather(j):
         slot = target_plane(j) * (inner * cap) + lax.broadcasted_iota(
             jnp.int32, (inner * cap, rows), 0
@@ -126,8 +165,14 @@
             block = jnp.dot(pick, high[:, columns], preferred_element_type=jnp.float32)
             block = block + jnp.dot(pick, low[:, columns], preferred_element_type=jnp.float32)
             out[j, c] = block.reshape(inner, cap, chunk)
-            for d in range(1, inner):
-                data_copy(j, c, d, False).start()
+            if j == 0 and c == 0:
+                pl.semaphore_wait(barrier, inner + outer - 2)
+            for d in (6, 7):
+                relay_out(j, c, d).start()
+            for d in (2, 3, 1):
+                data_copy(j, c, d).start()
+            if j * chunks + c < ahead:
+                own_y(j * chunks + c)
         if j == 0:
             value = points_ref[...]
             norms = jnp.sum(value * value, axis=1, keepdims=True)
@@ -170,7 +215,7 @@
 
     def reduce(j, c):
         for d in range(1, inner):
-            data_copy(j, c, d, True).wait_recv()
+            data_arrival(j, c, d).wait_recv()
         got[j, c, seat] = out[j, c, seat]
         stack = []
         for s in range(inner):
@@ -195,13 +240,20 @@
     low[...] = (value - top.astype(jnp.float32)).astype(jnp.bfloat16)
 
     gather(0)
+    passed = 0
+    for j in range(1, outer):
+        gather(j)
+        if j < outer - 1 and passed < steps:
+            pass_on(passed)
+            passed += 1
     behind = None
     for j in range(outer):
-        if j == 0:
-            for later in range(1, outer):
-                gather(later)
-        matches(j)
         for c in range(chunks):
+            while passed < min(j * chunks + c + 2, steps):
+                pass_on(passed)
+                passed += 1
+            if c == 0:
+                matches(j)
             reduce(j, c)
             if j < last:
                 @pl.when(jnp.logical_not(fed(j)))
@@ -231,7 +283,11 @@
         for d in range(1, inner):
             meta_copy(j, d, False).wait_send()
             for c in range(chunks):
-                data_copy(j, c, d, False).wait_send()
+                if d < 6:
+                    data_copy(j, c, d).wait_send()
+                else:
+                    relay_out(j, c, d).wait_send()
+                    relay_on(j, c, d).wait_send()
     for j in range(last):
         aux_copy(j, False).wait_send()
         for c in range(chunks):
@@ -242,9 +298,7 @@
     owners = lax.axis_size("dev")
     rows, width = points.shape
     cap = 2 * rows // owners
-    inner = 1
-    while 4 * inner * inner <= 2 * owners:
-        inner *= 2
+    inner = 8
     outer = owners // inner
     chunk = width // 3 if width % (3 * LANES) == 0 else width
     chunks = width // chunk
@@ -276,6 +330,7 @@
             pltpu.VMEM((CL_OWN, inner * LANES), b16),
             pltpu.VMEM((outer, chunks, inner, cap, chunk), f32),
             pltpu.VMEM((outer, chunks, inner, cap, chunk), f32),
+            pltpu.VMEM((outer, chunks, 2, cap, chunk), f32),
             pltpu.VMEM((outer, inner, 8, LANES), f32),
             pltpu.VMEM((outer, inner, 8, LANES), f32),
             pltpu.VMEM((hops, chunks, CL_OWN, chunk), f32),
@@ -284,6 +339,7 @@
             pltpu.VMEM((outer, 8, CL_OWN), f32),
             dma((outer, inner)), dma((outer, inner)),
             dma((outer, chunks, inner)), dma((outer, chunks, inner)),
+            dma((outer, chunks, 2)), dma((outer, chunks, 2)),
             dma((hops, chunks)), dma((outer + 1, chunks)),
             dma((hops,)), dma((outer,)),
         ],

time: 98.5 us -> 98.8 us (level)
  no operation moved by 1% of the time
where the time goes in v3:
time: 98.8 us; the launch traced here: 98.5 us
  Pallas kernels  91.8 us (93%)
  other arithmetic  5.57 us (6%)
    pallas_call x1, Pallas kernels, body(): pl.pallas_call(functools.partial(kernel, inner, outer, cap, chunk), out_s...  91.8 us
    reduce_sum x1, other arithmetic, finish(): jnp.sum(sums * sums, axis=1) / denom  2.14 us

profile of v3, /device:TPU:0, one launch (start us, length us, event | category | flops | bytes accessed | tf_op | source)
XLA Modules:
  0.0 98.5 jit_solution(5358547343816578232)
XLA Ops:
  0.6 0.7 add_select_fusion.1
  1.3 0.5 fusion.2
  1.9 0.7 convert_add_fusion
  2.6 0.6 pad_add_fusion.route_ref
  3.2 91.8 %shard_map.41 = (f32[256,768]{1,0:T(8,128)}, f32[8,256]{1,0:T(8,128)}) custom-call(f32[1024,768]{1,0:T(8,128)} %points_ref.1, s32[2,1024]{1,0:T(2,128)} %pad_add_fusion.route_ref), custom_call_target="tpu_custom_call" | custom-call | tf_op jit(solution)/shard_map/pallas_call | solution.py:318
  94.9 0.9 slice_add_fusion
  95.8 2.1 %multiply_reduce_fusion = (f32[256]{0:T(256)S(1)}, f32[256,768]{1,0:T(8,128)}) fusion(f32[256,768]{1,0:T(8,128)} %get-tuple-element.4, f32[256]{0:T(256)S(1)} %bitcast.6), kind=kLoop, calls=%fused_computation.4 | loop fusion | flops 589568 | bytes 1574912 | tf_op jit(solution)/shard_map/reduce_sum | solution.py:18
  97.9 0.6 multiply_divide_fusion

commit v4 on v3

--- a/solution.py
+++ b/solution.py
@@ -31,8 +31,8 @@
 def kernel(
     inner, outer, cap, chunk,
     points_ref, route_ref, sums_ref, aux_ref,
-    high, low, facts, hit, out, got, relay, mout, mgot, zout, zin, zaux, zin_aux,
-    msend, mrecv, send, recv, rsend, rrecv, zsend, zrecv, asend, arecv,
+    high, low, facts, hit, hold, cout, xin, yin, mout, mgot, zout, zin, zaux, zin_aux,
+    msend, mrecv, csend, crecv, xsend, xrecv, ysend, yrecv, zsend, zrecv, asend, arecv,
 ):
     me = lax.axis_index("dev")
     plane = me // inner
@@ -78,32 +78,39 @@
             device_id_type=MESH,
         )
 
-    def data_copy(j, c, d):
-        return plane_copy(
-            out.at[j, c, across(d)], got.at[j, c, seat], send.at[j, c, d], recv.at[j, c, d], d
-        )
-
-    def relay_out(j, c, d):
-        return plane_copy(
-            out.at[j, c, across(d)], relay.at[j, c, d - 6], rsend.at[j, c, d - 6],
-            rrecv.at[j, c, d - 6], 2,
-        )
-
-    def relay_on(j, c, d):
-        return plane_copy(
-            relay.at[j, c, d - 6], got.at[j, c, across(2)], send.at[j, c, d], recv.at[j, c, d],
-            d - 2,
-        )
-
-    def data_arrival(j, c, d):
-        return plane_copy(
-            out.at[j, c, 0], got.at[j, c, across(d)], send.at[j, c, d], recv.at[j, c, d], d
-        )
-
-    def meta_copy(j, d, arriving):
-        return plane_copy(
-            mout.at[j, across(d)], mgot.at[j, across(d) if arriving else seat],
-            msend.at[j, d], mrecv.at[j, d], d,
+    core = lax.rem(seat, 2)
+    x = lax.rem(seat // 2, 2)
+    y = seat // 4
+
+    def core_copy(t):
+        j, c = t // chunks, t % chunks
+        return plane_copy(
+            cout.at[j, c], hold.at[j, c, :, core], csend.at[j, c], crecv.at[j, c], 1
+        )
+
+    def core_arrival(t):
+        j, c = t // chunks, t % chunks
+        return plane_copy(
+            cout.at[j, c], hold.at[j, c, :, 1 - core], csend.at[j, c], crecv.at[j, c], 1
+        )
+
+    def x_copy(t):
+        j, c = t // chunks, t % chunks
+        return plane_copy(
+            hold.at[j, c, pl.ds((1 - x) * 2, 2)], xin.at[j, c], xsend.at[j, c], xrecv.at[j, c], 2
+        )
+
+    def y_copy(t, passed):
+        j, c = t // chunks, t % chunks
+        source = xin.at[j, c, 1 - y] if passed else hold.at[j, c, x * 2 + 1 - y]
+        return plane_copy(
+            source, yin.at[j, c, passed], ysend.at[j, c, passed], yrecv.at[j, c, passed], 4
+        )
+
+    def meta_copy(d, arriving):
+        return plane_copy(
+            mout.at[across(d)], mgot.at[across(d) if arriving else seat],
+            msend.at[d], mrecv.at[d], d,
         )
 
     def line_copy(j, c):
@@ -142,64 +149,66 @@
         )
 
     steps = outer * chunks
-    ahead = min(2, steps)
-
-    def own_y(t):
-        for d in (4, 5):
-            data_copy(t // chunks, t % chunks, d).start()
+    ahead = 3
+    half = inner // 2 * cap
+
+    def picks(j):
+        row = lax.broadcasted_iota(jnp.int32, (2 * half, 1), 0)
+        slot = target_plane(j) * (2 * half) + row
+        slot = slot + jnp.where(row < half, core * half, -core * half)
+        return (slot == route_ref[0:1, :]).astype(jnp.bfloat16)
+
+    def gather(t, pick):
+        j, c = t // chunks, t % chunks
+        columns = slice(c * chunk, (c + 1) * chunk)
+        block = jnp.dot(pick, high[:, columns], preferred_element_type=jnp.float32)
+        block = block + jnp.dot(pick, low[:, columns], preferred_element_type=jnp.float32)
+        hold[j, c, :, core] = block[:half].reshape(inner // 2, cap, chunk)
+        cout[j, c] = block[half:].reshape(inner // 2, cap, chunk)
+        if t == 0:
+            pl.semaphore_wait(barrier, inner + outer - 2)
+        core_copy(t).start()
+
+    def launch(t):
+        core_arrival(t).wait_recv()
+        x_copy(t).start()
+        y_copy(t, 0).start()
 
     def pass_on(t):
-        for d in (6, 7):
-            relay_out(t // chunks, t % chunks, d).wait_recv()
-            relay_on(t // chunks, t % chunks, d).start()
+        x_copy(t).wait_recv()
+        y_copy(t, 1).start()
         if t + ahead < steps:
-            own_y(t + ahead)
-
-    def gather(j):
-        slot = target_plane(j) * (inner * cap) + lax.broadcasted_iota(
-            jnp.int32, (inner * cap, rows), 0
-        )
-        pick = (slot == route_ref[0:1, :]).astype(jnp.bfloat16)
-        for c in range(chunks):
-            columns = slice(c * chunk, (c + 1) * chunk)
-            block = jnp.dot(pick, high[:, columns], preferred_element_type=jnp.float32)
-            block = block + jnp.dot(pick, low[:, columns], preferred_element_type=jnp.float32)
-            out[j, c] = block.reshape(inner, cap, chunk)
-            if j == 0 and c == 0:
-                pl.semaphore_wait(barrier, inner + outer - 2)
-            for d in (6, 7):
-                relay_out(j, c, d).start()
-            for d in (2, 3, 1):
-                data_copy(j, c, d).start()
-            if j * chunks + c < ahead:
-                own_y(j * chunks + c)
-        if j == 0:
-            value = points_ref[...]
-            norms = jnp.sum(value * value, axis=1, keepdims=True)
-            norms = jnp.broadcast_to(norms, (rows, LANES)).T[0:1, :]
-            label = route_ref[1:2, :].astype(jnp.float32).astype(jnp.bfloat16)
-            blank = jnp.zeros((4, rows), jnp.bfloat16)
-            facts[...] = jnp.concatenate([label] + pieces(norms, 3) + [blank], axis=0)
+            launch(t + ahead)
+
+    def tell():
+        value = points_ref[...]
+        norms = jnp.sum(value * value, axis=1, keepdims=True)
+        norms = jnp.broadcast_to(norms, (rows, LANES)).T[0:1, :]
+        label = route_ref[1:2, :].astype(jnp.float32).astype(jnp.bfloat16)
+        blank = jnp.zeros((4, rows), jnp.bfloat16)
+        facts[...] = jnp.concatenate([label] + pieces(norms, 3) + [blank], axis=0)
+
+    def tell_slots(j, pick):
         told = lax.dot_general(
             facts[...], pick, (((1,), (1,)), ((), ())), preferred_element_type=jnp.float32
         )
-        for p in range(inner):
-            mine = told[:, p * cap : (p + 1) * cap]
-            mout[j, p] = jnp.concatenate([mine] * rep, axis=1)
-        for d in range(1, inner):
-            meta_copy(j, d, False).start()
+        for q in range(inner):
+            p = q % 2 * 4 + q // 2 % 2 * 2 + (core if q < inner // 2 else 1 - core)
+            mine = told[:, q * cap : (q + 1) * cap]
+            mout[p, j] = jnp.concatenate([mine] * rep, axis=1)
 
     lane = lax.broadcasted_iota(jnp.int32, (8, LANES), 1)
     line = lax.broadcasted_iota(jnp.int32, (8, LANES), 0)
     cluster = lax.broadcasted_iota(jnp.int32, (CL_OWN, LANES), 0).astype(jnp.float32) + 1.0
 
     def matches(j):
-        for d in range(1, inner):
-            meta_copy(j, d, True).wait_recv()
-        mgot[j, seat] = mout[j, seat]
+        if j == 0:
+            for d in range(1, inner):
+                meta_copy(d, True).wait_recv()
+            mgot[seat] = mout[seat]
         weights = []
         for s in range(inner):
-            block = mgot[j, s]
+            block = mgot[across(s // 2 * 2) - core + s % 2, j]
             hit[:, s * LANES : (s + 1) * LANES] = (cluster == block[0:1, :]).astype(jnp.bfloat16)
             block = jnp.where(line == 0, 1.0, block)
             weights.append(jnp.where(lane < cap, block, 0.0).astype(jnp.bfloat16))
@@ -214,12 +223,13 @@
             aux_ref[...] = aux
 
     def reduce(j, c):
-        for d in range(1, inner):
-            data_arrival(j, c, d).wait_recv()
-        got[j, c, seat] = out[j, c, seat]
+        t = j * chunks + c
+        y_copy(t, 0).wait_recv()
+        y_copy(t, 1).wait_recv()
         stack = []
-        for s in range(inner):
-            stack.extend(pieces(got[j, c, s], rep))
+        for ref in (hold.at[j, c, x * 2 + y], xin.at[j, c, y], yin.at[j, c, 0], yin.at[j, c, 1]):
+            for s in range(2):
+                stack.extend(pieces(ref[s], rep))
         total = jnp.dot(hit[...], jnp.concatenate(stack, axis=0), preferred_element_type=jnp.float32)
         if j == last:
             sums_ref[:, c * chunk : (c + 1) * chunk] = total
@@ -239,11 +249,28 @@
     high[...] = top
     low[...] = (value - top.astype(jnp.float32)).astype(jnp.bfloat16)
 
-    gather(0)
+    pick = picks(0)
+    gather(0, pick)
+    tell()
+    launch(0)
+    for j in range(outer):
+        tell_slots(j, picks(j))
+    for d in range(1, inner):
+        meta_copy(d, False).start()
+    for t in range(1, chunks):
+        gather(t, pick)
+    for t in range(1, ahead):
+        if t < chunks:
+            launch(t)
     passed = 0
     for j in range(1, outer):
-        gather(j)
-        if j < outer - 1 and passed < steps:
+        pick = picks(j)
+        for c in range(chunks):
+            gather(j * chunks + c, pick)
+        if j == 1:
+            for t in range(chunks, ahead):
+                launch(t)
+        if j < outer - 1:
             pass_on(passed)
             passed += 1
     behind = None
@@ -279,15 +306,13 @@
             line_arrival(outer, c).wait_recv()
             sums_ref[:, columns] += zin[outer, c]
 
-    for j in range(outer):
-        for d in range(1, inner):
-            meta_copy(j, d, False).wait_send()
-            for c in range(chunks):
-                if d < 6:
-                    data_copy(j, c, d).wait_send()
-                else:
-                    relay_out(j, c, d).wait_send()
-                    relay_on(j, c, d).wait_send()
+    for d in range(1, inner):
+        meta_copy(d, False).wait_send()
+    for t in range(steps):
+        core_copy(t).wait_send()
+        x_copy(t).wait_send()
+        y_copy(t, 0).wait_send()
+        y_copy(t, 1).wait_send()
     for j in range(last):
         aux_copy(j, False).wait_send()
         for c in range(chunks):
@@ -309,7 +334,9 @@
     earlier = (jnp.arange(rows)[:, None] > jnp.arange(rows)[None, :]).astype(jnp.float32)
     before = jnp.dot(earlier, matches, preferred_element_type=jnp.float32)
     position = jnp.sum(before * matches, axis=1).astype(jnp.int32)
-    target = owner * cap + position
+    seat = owner % inner
+    place = owner - seat + seat % 2 * 4 + seat // 2 % 2 * 2 + seat // 4
+    target = place * cap + position
     route = jnp.stack([target, local_label + 1])
 
     f32, b16 = jnp.float32, jnp.bfloat16
@@ -328,17 +355,19 @@
             pltpu.VMEM((rows, width), b16),
             pltpu.VMEM((8, rows), b16),
             pltpu.VMEM((CL_OWN, inner * LANES), b16),
-            pltpu.VMEM((outer, chunks, inner, cap, chunk), f32),
-            pltpu.VMEM((outer, chunks, inner, cap, chunk), f32),
-            pltpu.VMEM((outer, chunks, 2, cap, chunk), f32),
-            pltpu.VMEM((outer, inner, 8, LANES), f32),
-            pltpu.VMEM((outer, inner, 8, LANES), f32),
+            pltpu.VMEM((outer, chunks, inner // 2, 2, cap, chunk), f32),
+            pltpu.VMEM((outer, chunks, inner // 2, cap, chunk), f32),
+            pltpu.VMEM((outer, chunks, 2, 2, cap, chunk), f32),
+            pltpu.VMEM((outer, chunks, 2, 2, cap, chunk), f32),
+            pltpu.VMEM((inner, outer, 8, LANES), f32),
+            pltpu.VMEM((inner, outer, 8, LANES), f32),
             pltpu.VMEM((hops, chunks, CL_OWN, chunk), f32),
             pltpu.VMEM((outer + 1, chunks, CL_OWN, chunk), f32),
             pltpu.VMEM((hops, 8, CL_OWN), f32),
             pltpu.VMEM((outer, 8, CL_OWN), f32),
-            dma((outer, inner)), dma((outer, inner)),
-            dma((outer, chunks, inner)), dma((outer, chunks, inner)),
+            dma((inner,)), dma((inner,)),
+            dma((outer, chunks)), dma((outer, chunks)),
+            dma((outer, chunks)), dma((outer, chunks)),
             dma((outer, chunks, 2)), dma((outer, chunks, 2)),
             dma((hops, chunks)), dma((outer + 1, chunks)),
             dma((hops,)), dma((outer,)),

time: 98.8 us -> 94.5 us (0.956)
  Pallas kernels: 91.8 us -> 87.5 us
    pallas_call x1, Pallas kernels: 91.8 us -> 87.5 us  [body(): pl.pallas_call(functools.partial(kernel, inner, outer, cap, chunk), out_s...]
where the time goes in v4:
time: 94.5 us; the launch traced here: 94.3 us
  Pallas kernels  87.5 us (93%)
  other arithmetic  5.6 us (6%)
    pallas_call x1, Pallas kernels, body(): pl.pallas_call(functools.partial(kernel, inner, outer, cap, chunk), out_s...  87.5 us
    reduce_sum x1, other arithmetic, finish(): jnp.sum(sums * sums, axis=1) / denom  2.14 us

profile of v4, /device:TPU:0, one launch (start us, length us, event | category | flops | bytes accessed | tf_op | source)
XLA Modules:
  0.0 94.3 jit_solution(15534615394409910641)
XLA Ops:
  0.6 0.7 add_select_fusion.6
  1.3 0.5 fusion.2
  1.9 0.7 fusion.10
  2.6 0.6 pad_add_fusion.route_ref
  3.2 87.5 %shard_map.41 = (f32[256,768]{1,0:T(8,128)}, f32[8,256]{1,0:T(8,128)}) custom-call(f32[1024,768]{1,0:T(8,128)} %points_ref.1, s32[2,1024]{1,0:T(2,128)} %pad_add_fusion.route_ref), custom_call_target="tpu_custom_call" | custom-call | tf_op jit(solution)/shard_map/pallas_call | solution.py:345
  90.7 0.9 slice_add_fusion
  91.5 2.1 %multiply_reduce_fusion = (f32[256]{0:T(256)S(1)}, f32[256,768]{1,0:T(8,128)}) fusion(f32[256,768]{1,0:T(8,128)} %get-tuple-element.4, f32[256]{0:T(256)S(1)} %bitcast.6), kind=kLoop, calls=%fused_computation.4 | loop fusion | flops 589568 | bytes 1574912 | tf_op jit(solution)/shard_map/reduce_sum | solution.py:18
  93.7 0.6 multiply_divide_fusion

commit v5 on v4

--- a/solution.py
+++ b/solution.py
@@ -149,7 +149,7 @@
         )
 
     steps = outer * chunks
-    ahead = 3
+    ahead = 2
     half = inner // 2 * cap
 
     def picks(j):

time: 94.5 us -> 94.5 us (level)
  no operation moved by 1% of the time
where the time goes in v5:
time: 94.5 us; the launch traced here: 94.3 us
  Pallas kernels  87.5 us (93%)
  other arithmetic  5.6 us (6%)
    pallas_call x1, Pallas kernels, body(): pl.pallas_call(functools.partial(kernel, inner, outer, cap, chunk), out_s...  87.5 us
    reduce_sum x1, other arithmetic, finish(): jnp.sum(sums * sums, axis=1) / denom  2.14 us

profile of v5, /device:TPU:0, one launch (start us, length us, event | category | flops | bytes accessed | tf_op | source)
XLA Modules:
  0.0 94.3 jit_solution(15400862962733729939)
XLA Ops:
  0.6 0.7 add_select_fusion.6
  1.3 0.5 fusion.2
  1.9 0.7 fusion.10
  2.6 0.6 pad_add_fusion.route_ref
  3.2 87.5 %shard_map.41 = (f32[256,768]{1,0:T(8,128)}, f32[8,256]{1,0:T(8,128)}) custom-call(f32[1024,768]{1,0:T(8,128)} %points_ref.1, s32[2,1024]{1,0:T(2,128)} %pad_add_fusion.route_ref), custom_call_target="tpu_custom_call" | custom-call | tf_op jit(solution)/shard_map/pallas_call | solution.py:345
  90.7 0.9 slice_add_fusion
  91.5 2.1 %multiply_reduce_fusion = (f32[256]{0:T(256)S(1)}, f32[256,768]{1,0:T(8,128)}) fusion(f32[256,768]{1,0:T(8,128)} %get-tuple-element.4, f32[256]{0:T(256)S(1)} %bitcast.6), kind=kLoop, calls=%fused_computation.4 | loop fusion | flops 589568 | bytes 1574912 | tf_op jit(solution)/shard_map/reduce_sum | solution.py:18
  93.7 0.6 multiply_divide_fusion
